TPU v7x, 32 devices: a whole 2x2x4 slice. The times are simulated.
32 devices in a mesh: gz: 2 (over core), row: 4 (over y, x), col: 4 (over z).
Axes of the slice: x: 2, y: 2, z: 4, core: 2. Of those that a mesh axis runs over, the one named last changes fastest.
Arguments:
- right_sides: float32 [32, 4, 16, 256], P(('gz', 'row', 'col')), may hold values from -6 to 6
- lower_inverse: bfloat16 [32, 4, 256, 256], P(('gz', 'row', 'col')), may hold values from -0.375 to 0.375
- upper_inverse: bfloat16 [32, 4, 256, 256], P(('gz', 'row', 'col')), may hold values from -0.375 to 0.375
- lower_blocks: bfloat16 [32, 4, 2, 256, 256], P(('gz', 'row', 'col')), may hold values from -0.125 to 0.125
- upper_blocks: bfloat16 [32, 4, 2, 256, 256], P(('gz', 'row', 'col')), may hold values from -0.125 to 0.125
- node_widths: int32 [32, 4], P(('gz', 'row', 'col')), may hold values from 128 to 256, as said below
- far_levels: int32 [32, 4], P(('gz', 'row', 'col')), may hold values from 0 to 5, as said below
- owner_level: int32 [32], replicated, may hold values from 0 to 5, as said below
Outputs:
- solution: float32 [32, 4, 16, 256], P(('gz', 'row', 'col'))
Inputs may be any that keep to these rules, and one draw needn't show every extreme that they name: Columns c >= node_widths of a supernode are padding; every device holds a supernode with all 256 columns. `far_levels`: between 2 and 5 where the supernode has two or more ancestors, but never past the root; 1 where it has one; 0 for the root and for the slot of the device that owns no separator. `owner_level`: every separator of level u is owned by exactly one device of its group (the devices t with the same t // 2**u); one device owns none and holds 0.
All inputs are finite; a program needn't handle non-finite values.
Results may differ from a plain program's by a relative error of at most 0.018.
Values may be sent and summed in bfloat16 or wider, within the bound.
A program may use at most 64 MiB of HBM per device.

v0:
```python
import jax
import jax.numpy as jnp
from jax import lax
from jax.sharding import PartitionSpec as P

W = 256
RHS = 16
NB = 2
LOCAL_LEVELS = 2
LOCAL_COUNT = 3


def level_start(height):
    return 2**LOCAL_LEVELS - 2 ** (LOCAL_LEVELS - height)


def apply_blocks(vectors, blocks):
    return jnp.einsum("snrk,snak->snra", vectors, blocks, preferred_element_type=jnp.float32)


def apply_single(vectors, blocks):
    return jnp.einsum("srk,sak->sra", vectors, blocks, preferred_element_type=jnp.float32)


def forward_local(right_sides, lower_inverse, lower_blocks, padding, far_levels, upper_levels):
    batch_size = right_sides.shape[0]
    pending = jnp.zeros((batch_size, LOCAL_COUNT, RHS, W), jnp.float32)
    upper_pending = jnp.zeros((batch_size, upper_levels, RHS, W), jnp.float32)
    solved = []
    for height in range(LOCAL_LEVELS):
        offset = level_start(height)
        amount = 2 ** (LOCAL_LEVELS - 1 - height)
        residue = (
            right_sides[:, offset : offset + amount] - pending[:, offset : offset + amount]
        ).astype(jnp.bfloat16)
        solved_now = padding[:, offset : offset + amount] * apply_blocks(
            residue, lower_inverse[:, offset : offset + amount]
        )
        solved.append(solved_now)
        rounded = solved_now.astype(jnp.bfloat16)
        for block_id in range(NB):
            product = apply_blocks(rounded, lower_blocks[:, offset : offset + amount, block_id])
            for distance in range(1, upper_levels + 1):
                if block_id == 0 and distance > 1:
                    continue
                if block_id == 0:
                    chosen = product
                else:
                    matches = far_levels[:, offset : offset + amount] == distance
                    chosen = jnp.where(matches[:, :, None, None], product, 0.0)
                target = height + distance
                if target < LOCAL_LEVELS:
                    target_count = amount // 2**distance
                    folded = chosen.reshape(batch_size, target_count, 2**distance, RHS, W).sum(
                        axis=2
                    )
                    begin_at = level_start(target)
                    pending = pending.at[:, begin_at : begin_at + target_count].add(folded)
                else:
                    upper_pending = upper_pending.at[:, target - LOCAL_LEVELS].add(
                        chosen.sum(axis=1)
                    )
    return (jnp.concatenate(solved, axis=1), upper_pending)


def backward_local(forward, upper_inverse, upper_blocks, padding, far_levels, upper_known):
    upper_levels = upper_known.shape[1]
    solutions = [None] * LOCAL_LEVELS
    for height in reversed(range(LOCAL_LEVELS)):
        offset = level_start(height)
        amount = 2 ** (LOCAL_LEVELS - 1 - height)
        residue = forward[:, offset : offset + amount]
        for block_id in range(NB):
            operand = jnp.zeros(residue.shape, jnp.float32)
            for distance in range(1, upper_levels + 1):
                if block_id == 0 and distance > 1:
                    continue
                target = height + distance
                if target < LOCAL_LEVELS:
                    known_part = jnp.repeat(solutions[target], 2**distance, axis=1)
                else:
                    known_part = jnp.broadcast_to(
                        upper_known[:, target - LOCAL_LEVELS][:, None], residue.shape
                    )
                if block_id == 0:
                    operand = known_part
                else:
                    matches = far_levels[:, offset : offset + amount] == distance
                    operand = operand + jnp.where(matches[:, :, None, None], known_part, 0.0)
            residue = residue - apply_blocks(
                operand.astype(jnp.bfloat16), upper_blocks[:, offset : offset + amount, block_id]
            )
        solutions[height] = padding[:, offset : offset + amount] * apply_blocks(
            residue.astype(jnp.bfloat16), upper_inverse[:, offset : offset + amount]
        )
    return jnp.concatenate(solutions, axis=1)


def spread_slots(partial_value, slot_count, slot_at):
    chosen = (jnp.arange(slot_count, dtype=jnp.int32) == slot_at)[:, None, None]
    return jnp.where(chosen, partial_value, 0.0)


def group_total(partial_value, height, layout, places):
    col_levels, grid_levels, col_span, grid_span, total_span = layout
    if height <= col_levels:
        slot_at = places[0] // 2**height
        summed = lax.psum(
            spread_slots(partial_value, col_span // 2**height, slot_at).astype(jnp.bfloat16), "col"
        ).astype(jnp.float32)
    elif height <= grid_levels:
        slot_at = places[1] // 2**height
        summed = lax.psum(
            spread_slots(partial_value, grid_span // 2**height, slot_at), ("row", "col")
        )
    else:
        slot_at = places[2] // 2**height
        summed = lax.psum(
            spread_slots(partial_value, total_span // 2**height, slot_at), ("gz", "row", "col")
        )
    return lax.dynamic_index_in_dim(summed, slot_at, 0, keepdims=True)


def group_share(partial_value, height, layout, places):
    col_levels, grid_levels, col_span, grid_span, total_span = layout
    if height <= col_levels:
        slot_at = places[0] // 2**height
        summed = lax.psum(
            spread_slots(partial_value, col_span // 2**height, slot_at).astype(jnp.bfloat16), "col"
        ).astype(jnp.float32)
    elif height <= grid_levels:
        slot_at = places[1] // 2**height
        summed = lax.psum(
            spread_slots(partial_value, grid_span // 2**height, slot_at), ("row", "col")
        )
    else:
        slot_at = places[2] // 2**height
        summed = lax.psum(
            spread_slots(partial_value, total_span // 2**height, slot_at), ("gz", "row", "col")
        )
    return lax.dynamic_index_in_dim(summed, slot_at, 0, keepdims=True)


def local(
    right_sides,
    lower_inverse,
    upper_inverse,
    lower_blocks,
    upper_blocks,
    node_widths,
    far_levels,
    owner_level,
):
    col_span = lax.axis_size("col")
    row_span = lax.axis_size("row")
    layer_span = lax.axis_size("gz")
    col_levels = col_span.bit_length() - 1
    grid_levels = col_levels + row_span.bit_length() - 1
    upper_levels = grid_levels + layer_span.bit_length() - 1
    col_place = lax.axis_index("col")
    grid_place = lax.axis_index("row") * col_span + col_place
    device = lax.axis_index("gz") * row_span * col_span + grid_place
    layout = (
        col_levels,
        grid_levels,
        col_span,
        row_span * col_span,
        layer_span * row_span * col_span,
    )
    places = (col_place, grid_place, device)
    columns = jnp.arange(W, dtype=jnp.int32)
    padding = (columns[None, None, None, :] < node_widths[:, :, None, None]).astype(jnp.float32)
    forward_nodes, upper_pending = forward_local(
        right_sides[:, :LOCAL_COUNT],
        lower_inverse[:, :LOCAL_COUNT],
        lower_blocks[:, :LOCAL_COUNT],
        padding[:, :LOCAL_COUNT],
        far_levels[:, :LOCAL_COUNT],
        upper_levels,
    )
    own_rights = right_sides[:, LOCAL_COUNT]
    own_padding = padding[:, LOCAL_COUNT]
    own_far = far_levels[:, LOCAL_COUNT]
    my_level = lax.dynamic_index_in_dim(owner_level, device, 0, keepdims=False)
    own_forward = jnp.zeros((1, RHS, W), jnp.float32)
    for height in range(1, upper_levels + 1):
        gathered = group_total(upper_pending[:, height - 1], height, layout, places)
        owner_here = my_level == height
        residue = (own_rights - gathered).astype(jnp.bfloat16)
        solved_now = jnp.where(
            owner_here, own_padding * apply_single(residue, lower_inverse[:, LOCAL_COUNT]), 0.0
        )
        own_forward = own_forward + solved_now
        rounded = solved_now.astype(jnp.bfloat16)
        for block_id in range(NB):
            product = apply_single(rounded, lower_blocks[:, LOCAL_COUNT, block_id])
            for distance in range(1, upper_levels + 1):
                if block_id == 0 and distance > 1:
                    continue
                target = height + distance
                if target > upper_levels:
                    continue
                if block_id == 0:
                    chosen = product
                else:
                    chosen = jnp.where((own_far == distance)[:, None, None], product, 0.0)
                upper_pending = upper_pending.at[:, target - 1].add(chosen)
    upper_known = jnp.zeros((1, upper_levels, RHS, W), jnp.float32)
    own_solution = jnp.zeros((1, RHS, W), jnp.float32)
    for height in range(upper_levels, 0, -1):
        owner_here = my_level == height
        residue = own_forward
        for block_id in range(NB):
            operand = jnp.zeros((1, RHS, W), jnp.float32)
            for distance in range(1, upper_levels + 1):
                if block_id == 0 and distance > 1:
                    continue
                target = height + distance
                if target > upper_levels:
                    continue
                known_part = upper_known[:, target - 1]
                if block_id == 0:
                    operand = known_part
                else:
                    operand = operand + jnp.where(
                        (own_far == distance)[:, None, None], known_part, 0.0
                    )
            residue = residue - apply_single(
                operand.astype(jnp.bfloat16), upper_blocks[:, LOCAL_COUNT, block_id]
            )
        solved_now = jnp.where(
            owner_here,
            own_padding * apply_single(residue.astype(jnp.bfloat16), upper_inverse[:, LOCAL_COUNT]),
            0.0,
        )
        own_solution = own_solution + solved_now
        shared = group_share(solved_now, height, layout, places)
        upper_known = upper_known.at[:, height - 1].set(shared)
    local_solution = backward_local(
        forward_nodes,
        upper_inverse[:, :LOCAL_COUNT],
        upper_blocks[:, :LOCAL_COUNT],
        padding[:, :LOCAL_COUNT],
        far_levels[:, :LOCAL_COUNT],
        upper_known,
    )
    return jnp.concatenate([local_solution, own_solution[:, None]], axis=1)


def solution(mesh):
    return jax.shard_map(
        local,
        mesh=mesh,
        in_specs=(
            P(("gz", "row", "col"), None, None, None),
            P(("gz", "row", "col"), None, None, None),
            P(("gz", "row", "col"), None, None, None),
            P(("gz", "row", "col"), None, None, None, None),
            P(("gz", "row", "col"), None, None, None, None),
            P(("gz", "row", "col"), None),
            P(("gz", "row", "col"), None),
            P(),
        ),
        out_specs=P(("gz", "row", "col"), None, None, None),
        check_vma=False,
    )
```

profile of v0, /device:TPU:0, one launch (start us, length us, event | category | flops | bytes accessed | tf_op | source)
XLA Modules:
  0.0 453.6 jit_solution(13407759819667578866)
XLA Ops:
  0.0 0.0 copy-start.1
  0.0 0.7 compare_bitcast_fusion.3
  0.8 0.7 fusion.307
  1.5 1.1 convolution_multiply_fusion.1
  2.6 1.2 select_reduce_fusion.4
  3.9 0.0 copy-start.2
  3.9 1.4 convolution_multiply_fusion.13
  5.3 0.0 copy-done.1
  5.3 0.2 fusion.24
  5.5 0.0 copy-start.5
  5.5 0.7 copy-done.5
  6.1 0.6 fusion.324
  7.4 0.2 fusion.167
  10.1 0.0 copy-start.4
  10.1 0.1 select_convert_fusion.1
  10.2 20.5 %psum.70 = bf16[2,16,256]{2,1,0:T(8,128)(2,1)S(1)} all-reduce(bf16[2,16,256]{2,1,0:T(8,128)(2,1)S(1)} %select_convert_fusion.1), channel_id=1, replica_groups=mesh['gz'=2,'row'=4,'col'=4] {'col'}, use_global_device_ids=true, to_apply=%region_5.6 | all-reduce | flops 8192 | bytes 32768 | tf_op jit(solution)/shard_map/psum | solution.py:108
  30.7 0.0 copy-start.6
  30.7 0.7 copy-done.6
  31.4 0.6 dynamic_slice.24
  32.7 0.0 copy-done.2
  32.7 0.0 copy-done.4
  32.7 0.2 fusion.23
  32.8 0.2 fusion.22
  33.7 0.2 fusion.166
  35.9 8.5 %psum.71 = bf16[1,16,256]{2,1,0:T(8,128)(2,1)S(1)} all-reduce(bf16[1,16,256]{2,1,0:T(8,128)(2,1)S(1)} %fusion.218), channel_id=1, replica_groups=mesh['gz'=2,'row'=4,'col'=4] {'col'}, use_global_device_ids=true, to_apply=%region_6.7 | all-reduce | flops 4096 | bytes 16384 | tf_op jit(solution)/shard_map/psum | solution.py:108
  45.1 0.2 fusion.21
  45.2 0.2 fusion.20
  45.4 0.2 fusion.165
  45.7 0.1 broadcast_select_fusion.1
  45.8 75.8 %psum.72 = f32[2,16,256]{2,1,0:T(8,128)S(1)} all-reduce(f32[2,16,256]{2,1,0:T(8,128)S(1)} %broadcast_select_fusion.1), channel_id=1, replica_groups=mesh['gz'=2,'row'=4,'col'=4] {'row','col'}, use_global_device_ids=true, to_apply=%region_7.8 | all-reduce | flops 8192 | bytes 65536 | tf_op jit(solution)/shard_map/psum | solution.py:113
  122.3 0.2 fusion.19
  122.4 0.2 fusion.78
  122.6 0.2 fusion.18
  122.8 72.1 %psum.73 = f32[1,16,256]{2,1,0:T(8,128)S(1)} all-reduce(f32[1,16,256]{2,1,0:T(8,128)S(1)} %fusion.18), channel_id=1, replica_groups=mesh['gz'=2,'row'=4,'col'=4] {'row','col'}, use_global_device_ids=true, to_apply=%region_8.9 | all-reduce | flops 4096 | bytes 32768 | tf_op jit(solution)/shard_map/psum | solution.py:113
  195.5 0.0 copy-start.3
  195.5 0.2 fusion.14
  195.7 0.2 fusion.13
  195.9 0.2 fusion.12
  196.0 36.9 %psum.74 = f32[1,16,256]{2,1,0:T(8,128)S(1)} all-reduce(f32[1,16,256]{2,1,0:T(8,128)S(1)} %fusion.12), channel_id=1, replica_groups=mesh['gz'=2,'row'=4,'col'=4] {'gz','row','col'}, use_global_device_ids=true, to_apply=%region_9.10 | all-reduce | flops 4096 | bytes 32768 | tf_op jit(solution)/shard_map/psum | solution.py:118
  233.6 0.2 fusion.8
  233.7 0.0 copy-done
  233.7 0.2 convolution_subtract_fusion.13
  233.9 0.0 copy-done.3
  233.9 0.3 fusion.6
  234.3 41.4 %psum.75 = f32[1,16,256]{2,1,0:T(8,128)S(1)} all-reduce(f32[1,16,256]{2,1,0:T(8,128)S(1)} %select_bitcast_fusion.1), channel_id=1, replica_groups=mesh['gz'=2,'row'=4,'col'=4] {'gz','row','col'}, use_global_device_ids=true, to_apply=%region_10.11 | all-reduce | flops 4096 | bytes 32768 | tf_op jit(solution)/shard_map/psum | solution.py:138
  275.7 0.1 convolution_subtract_fusion.11
  275.9 0.3 fusion.5
  276.2 76.1 %psum.76 = f32[1,16,256]{2,1,0:T(8,128)S(1)} all-reduce(f32[1,16,256]{2,1,0:T(8,128)S(1)} %select_bitcast_fusion), channel_id=1, replica_groups=mesh['gz'=2,'row'=4,'col'=4] {'row','col'}, use_global_device_ids=true, to_apply=%region_11.12 | all-reduce | flops 4096 | bytes 32768 | tf_op jit(solution)/shard_map/psum | solution.py:133
  352.3 0.1 convolution_subtract_fusion.9
  352.5 0.3 fusion.4
  352.8 0.1 broadcast_select_fusion
  352.9 72.1 %psum.77 = f32[2,16,256]{2,1,0:T(8,128)S(1)} all-reduce(f32[2,16,256]{2,1,0:T(8,128)S(1)} %broadcast_select_fusion), channel_id=1, replica_groups=mesh['gz'=2,'row'=4,'col'=4] {'row','col'}, use_global_device_ids=true, to_apply=%region_12.13 | all-reduce | flops 8192 | bytes 65536 | tf_op jit(solution)/shard_map/psum | solution.py:133
  425.0 0.1 convolution_subtract_fusion.7
  425.1 0.3 fusion.3
  425.4 8.5 %psum.78 = bf16[1,16,256]{2,1,0:T(8,128)(2,1)S(1)} all-reduce(bf16[1,16,256]{2,1,0:T(8,128)(2,1)S(1)} %fusion.201), channel_id=1, replica_groups=mesh['gz'=2,'row'=4,'col'=4] {'col'}, use_global_device_ids=true, to_apply=%region_13.14 | all-reduce | flops 4096 | bytes 16384 | tf_op jit(solution)/shard_map/psum | solution.py:128
  434.0 0.2 convolution_subtract_fusion.5
  434.1 0.3 fusion.2
  434.4 0.1 select_convert_fusion
  434.5 17.4 %psum.79 = bf16[2,16,256]{2,1,0:T(8,128)(2,1)S(1)} all-reduce(bf16[2,16,256]{2,1,0:T(8,128)(2,1)S(1)} %select_convert_fusion), channel_id=1, replica_groups=mesh['gz'=2,'row'=4,'col'=4] {'col'}, use_global_device_ids=true, to_apply=%region_14.15 | all-reduce | flops 8192 | bytes 32768 | tf_op jit(solution)/shard_map/psum | solution.py:128
  451.9 0.2 convolution_subtract_fusion.3
  452.1 0.3 fusion.325
  452.4 0.2 convolution_subtract_fusion.1
  452.6 0.3 fusion
  453.0 0.6 pad_maximum_fusion
  (33 shorter events, 0.2 us)
Async XLA Ops:
  0.0 5.3 %copy-start.1 = (bf16[1,4,2,256,256]{4,3,2,1,0:T(8,128)(2,1)S(1)}, bf16[1,4,2,256,256]{4,3,2,1,0:T(8,128)(2,1)}, u32[]{:S(2)}) copy-start(bf16[1,4,2,256,256]{4,3,2,1,0:T(8,128)(2,1)} %param.73) | copy-start | bytes 3145732
  3.9 28.8 %copy-start.2 = (bf16[1,4,256,256]{3,2,1,0:T(8,128)(2,1)S(1)}, bf16[1,4,256,256]{3,2,1,0:T(8,128)(2,1)}, u32[]{:S(2)}) copy-start(bf16[1,4,256,256]{3,2,1,0:T(8,128)(2,1)} %param.71) | copy-start | bytes 1572868
  5.5 0.7 copy-start.5
  10.1 22.6 %copy-start.4 = (f32[1,4,16,256]{3,2,1,0:T(8,128)S(1)}, f32[1,4,16,256]{3,2,1,0:T(8,128)}, u32[]{:S(2)}) copy-start(f32[1,4,16,256]{3,2,1,0:T(8,128)} %param.70) | copy-start | bytes 196612
  30.7 0.7 copy-start.6
  45.4 188.3 %copy-start = (bf16[1,4,2,256,256]{4,3,2,1,0:T(8,128)(2,1)S(1)}, bf16[1,4,2,256,256]{4,3,2,1,0:T(8,128)(2,1)}, u32[]{:S(2)}) copy-start(bf16[1,4,2,256,256]{4,3,2,1,0:T(8,128)(2,1)} %param.74) | copy-start | bytes 3145732
  195.5 38.4 %copy-start.3 = (bf16[1,4,256,256]{3,2,1,0:T(8,128)(2,1)S(1)}, bf16[1,4,256,256]{3,2,1,0:T(8,128)(2,1)}, u32[]{:S(2)}) copy-start(bf16[1,4,256,256]{3,2,1,0:T(8,128)(2,1)} %param.72) | copy-start | bytes 1572868
where the time goes:
time: 454 us
  blocking collectives  429 us (94%)
  matrix products  9.61 us (2%)
  between operations  9.28 us (2%)
    psum x2, blocking collectives, group_share(): lax.psum(spread_slots(partial_value, grid_span // 2 ** height, slot_at),...  148 us
    psum x2, blocking collectives, group_total(): lax.psum(spread_slots(partial_value, grid_span // 2 ** height, slot_at),...  148 us
    psum x1, blocking collectives, group_share(): lax.psum(spread_slots(partial_value, total_span // 2 ** height, slot_at),...  41.4 us
    psum x1, blocking collectives, group_total(): lax.psum(spread_slots(partial_value, total_span // 2 ** height, slot_at),...  36.9 us
    psum x2, blocking collectives, group_total(): lax.psum(spread_slots(partial_value, col_span // 2 ** height, slot_at).as...  29 us
    psum x2, blocking collectives, group_share(): lax.psum(spread_slots(partial_value, col_span // 2 ** height, slot_at).as...  25.9 us

commit v1 on v0

--- a/solution.py
+++ b/solution.py
@@ -136,7 +136,8 @@
     else:
         slot_at = places[2] // 2**height
         summed = lax.psum(
-            spread_slots(partial_value, total_span // 2**height, slot_at), ("gz", "row", "col")
+            lax.psum(spread_slots(partial_value, total_span // 2**height, slot_at), ("row", "col")),
+            "gz",
         )
     return lax.dynamic_index_in_dim(summed, slot_at, 0, keepdims=True)
 

time: 454 us -> 488 us (1.075)
  blocking collectives: 429 us -> 463 us
    psum x1, blocking collectives: 41.4 us -> 76 us  [group_share(): lax.psum(spread_slots(partial_value, total_span // 2 ** height, slot_at),...]
where the time goes in v1:
time: 488 us
  blocking collectives  463 us (95%)
  matrix products  9.61 us (2%)
  between operations  9.28 us (2%)
    psum x2, blocking collectives, group_total(): lax.psum(spread_slots(partial_value, grid_span // 2 ** height, slot_at),...  148 us
    psum x2, blocking collectives, group_share(): lax.psum(spread_slots(partial_value, grid_span // 2 ** height, slot_at),...  144 us
    psum x1, blocking collectives, group_share(): lax.psum(spread_slots(partial_value, total_span // 2 ** height, slot_at),...  76 us
    psum x1, blocking collectives, group_total(): lax.psum(spread_slots(partial_value, total_span // 2 ** height, slot_at),...  36.9 us
    psum x2, blocking collectives, group_total(): lax.psum(spread_slots(partial_value, col_span // 2 ** height, slot_at).as...  29 us
    psum x2, blocking collectives, group_share(): lax.psum(spread_slots(partial_value, col_span // 2 ** height, slot_at).as...  25.9 us

profile of v1, /device:TPU:0, one launch (start us, length us, event | category | flops | bytes accessed | tf_op | source)
XLA Modules:
  0.0 487.5 jit_solution(6717787891907760853)
XLA Ops:
  0.0 0.0 copy-start.1
  0.0 0.7 compare_bitcast_fusion.3
  0.8 0.7 fusion.307
  1.5 1.1 convolution_multiply_fusion.1
  2.6 1.2 select_reduce_fusion.4
  3.9 0.0 copy-start.2
  3.9 1.4 convolution_multiply_fusion.13
  5.3 0.0 copy-done.1
  5.3 0.2 fusion.24
  5.5 0.0 copy-start.5
  5.5 0.7 copy-done.5
  6.1 0.6 fusion.324
  7.4 0.2 fusion.167
  10.1 0.0 copy-start.4
  10.1 0.1 select_convert_fusion.1
  10.2 20.5 %psum.77 = bf16[2,16,256]{2,1,0:T(8,128)(2,1)S(1)} all-reduce(bf16[2,16,256]{2,1,0:T(8,128)(2,1)S(1)} %select_convert_fusion.1), channel_id=1, replica_groups=mesh['gz'=2,'row'=4,'col'=4] {'col'}, use_global_device_ids=true, to_apply=%region_5.6 | all-reduce | flops 8192 | bytes 32768 | tf_op jit(solution)/shard_map/psum | solution.py:108
  30.7 0.7 copy-done.6
  31.4 0.6 dynamic_slice.24
  32.7 0.0 copy-done.2
  32.7 0.0 copy-done.4
  32.7 0.2 fusion.23
  32.8 0.2 fusion.22
  33.7 0.2 fusion.166
  35.9 8.5 %psum.78 = bf16[1,16,256]{2,1,0:T(8,128)(2,1)S(1)} all-reduce(bf16[1,16,256]{2,1,0:T(8,128)(2,1)S(1)} %fusion.218), channel_id=1, replica_groups=mesh['gz'=2,'row'=4,'col'=4] {'col'}, use_global_device_ids=true, to_apply=%region_6.7 | all-reduce | flops 4096 | bytes 16384 | tf_op jit(solution)/shard_map/psum | solution.py:108
  45.1 0.2 fusion.21
  45.2 0.2 fusion.20
  45.4 0.2 fusion.165
  45.7 0.1 broadcast_select_fusion.1
  45.8 75.8 %psum.79 = f32[2,16,256]{2,1,0:T(8,128)S(1)} all-reduce(f32[2,16,256]{2,1,0:T(8,128)S(1)} %broadcast_select_fusion.1), channel_id=1, replica_groups=mesh['gz'=2,'row'=4,'col'=4] {'row','col'}, use_global_device_ids=true, to_apply=%region_7.8 | all-reduce | flops 8192 | bytes 65536 | tf_op jit(solution)/shard_map/psum | solution.py:113
  122.3 0.2 fusion.19
  122.4 0.2 fusion.78
  122.6 0.2 fusion.18
  122.8 72.1 %psum.80 = f32[1,16,256]{2,1,0:T(8,128)S(1)} all-reduce(f32[1,16,256]{2,1,0:T(8,128)S(1)} %fusion.18), channel_id=1, replica_groups=mesh['gz'=2,'row'=4,'col'=4] {'row','col'}, use_global_device_ids=true, to_apply=%region_8.9 | all-reduce | flops 4096 | bytes 32768 | tf_op jit(solution)/shard_map/psum | solution.py:113
  195.5 0.0 copy-start.3
  195.5 0.2 fusion.14
  195.7 0.2 fusion.13
  195.9 0.2 fusion.12
  196.0 36.9 %psum.81 = f32[1,16,256]{2,1,0:T(8,128)S(1)} all-reduce(f32[1,16,256]{2,1,0:T(8,128)S(1)} %fusion.12), channel_id=1, replica_groups=mesh['gz'=2,'row'=4,'col'=4] {'gz','row','col'}, use_global_device_ids=true, to_apply=%region_9.10 | all-reduce | flops 4096 | bytes 32768 | tf_op jit(solution)/shard_map/psum | solution.py:118
  233.6 0.2 fusion.8
  233.7 0.0 copy-done
  233.7 0.2 convolution_subtract_fusion.13
  233.9 0.0 copy-done.3
  233.9 0.3 fusion.6
  234.3 76.0 %psum.82 = f32[1,16,256]{2,1,0:T(8,128)S(1)} all-reduce(f32[1,16,256]{2,1,0:T(8,128)S(1)} %select_bitcast_fusion.1), channel_id=1, replica_groups=mesh['gz'=2,'row'=4,'col'=4] {'row','col'}, use_global_device_ids=true, to_apply=%region_10.11 | all-reduce | flops 4096 | bytes 32768 | tf_op jit(solution)/shard_map/psum | solution.py:139
  310.3 3.3 psum.83
  313.6 0.1 convolution_subtract_fusion.11
  313.8 0.3 fusion.5
  314.1 72.1 %psum.84 = f32[1,16,256]{2,1,0:T(8,128)S(1)} all-reduce(f32[1,16,256]{2,1,0:T(8,128)S(1)} %select_bitcast_fusion), channel_id=1, replica_groups=mesh['gz'=2,'row'=4,'col'=4] {'row','col'}, use_global_device_ids=true, to_apply=%region_12.13 | all-reduce | flops 4096 | bytes 32768 | tf_op jit(solution)/shard_map/psum | solution.py:133
  386.2 0.1 convolution_subtract_fusion.9
  386.4 0.3 fusion.4
  386.7 0.1 broadcast_select_fusion
  386.8 72.1 %psum.85 = f32[2,16,256]{2,1,0:T(8,128)S(1)} all-reduce(f32[2,16,256]{2,1,0:T(8,128)S(1)} %broadcast_select_fusion), channel_id=1, replica_groups=mesh['gz'=2,'row'=4,'col'=4] {'row','col'}, use_global_device_ids=true, to_apply=%region_13.14 | all-reduce | flops 8192 | bytes 65536 | tf_op jit(solution)/shard_map/psum | solution.py:133
  458.9 0.1 convolution_subtract_fusion.7
  459.1 0.3 fusion.3
  459.4 8.5 %psum.86 = bf16[1,16,256]{2,1,0:T(8,128)(2,1)S(1)} all-reduce(bf16[1,16,256]{2,1,0:T(8,128)(2,1)S(1)} %fusion.201), channel_id=1, replica_groups=mesh['gz'=2,'row'=4,'col'=4] {'col'}, use_global_device_ids=true, to_apply=%region_14.15 | all-reduce | flops 4096 | bytes 16384 | tf_op jit(solution)/shard_map/psum | solution.py:128
  467.9 0.2 convolution_subtract_fusion.5
  468.1 0.3 fusion.2
  468.4 0.1 select_convert_fusion
  468.5 17.4 %psum.87 = bf16[2,16,256]{2,1,0:T(8,128)(2,1)S(1)} all-reduce(bf16[2,16,256]{2,1,0:T(8,128)(2,1)S(1)} %select_convert_fusion), channel_id=1, replica_groups=mesh['gz'=2,'row'=4,'col'=4] {'col'}, use_global_device_ids=true, to_apply=%region_15.16 | all-reduce | flops 8192 | bytes 32768 | tf_op jit(solution)/shard_map/psum | solution.py:128
  485.9 0.2 convolution_subtract_fusion.3
  486.0 0.3 fusion.325
  486.4 0.2 convolution_subtract_fusion.1
  486.6 0.3 fusion
  486.9 0.6 pad_maximum_fusion
  (34 shorter events, 0.2 us)
Async XLA Ops:
  0.0 5.3 %copy-start.1 = (bf16[1,4,2,256,256]{4,3,2,1,0:T(8,128)(2,1)S(1)}, bf16[1,4,2,256,256]{4,3,2,1,0:T(8,128)(2,1)}, u32[]{:S(2)}) copy-start(bf16[1,4,2,256,256]{4,3,2,1,0:T(8,128)(2,1)} %param.73) | copy-start | bytes 3145732
  3.9 28.8 %copy-start.2 = (bf16[1,4,256,256]{3,2,1,0:T(8,128)(2,1)S(1)}, bf16[1,4,256,256]{3,2,1,0:T(8,128)(2,1)}, u32[]{:S(2)}) copy-start(bf16[1,4,256,256]{3,2,1,0:T(8,128)(2,1)} %param.71) | copy-start | bytes 1572868
  5.5 0.7 copy-start.5
  10.1 22.6 %copy-start.4 = (f32[1,4,16,256]{3,2,1,0:T(8,128)S(1)}, f32[1,4,16,256]{3,2,1,0:T(8,128)}, u32[]{:S(2)}) copy-start(f32[1,4,16,256]{3,2,1,0:T(8,128)} %param.70) | copy-start | bytes 196612
  30.7 0.7 copy-start.6
  45.4 188.3 %copy-start = (bf16[1,4,2,256,256]{4,3,2,1,0:T(8,128)(2,1)S(1)}, bf16[1,4,2,256,256]{4,3,2,1,0:T(8,128)(2,1)}, u32[]{:S(2)}) copy-start(bf16[1,4,2,256,256]{4,3,2,1,0:T(8,128)(2,1)} %param.74) | copy-start | bytes 3145732
  195.5 38.4 %copy-start.3 = (bf16[1,4,256,256]{3,2,1,0:T(8,128)(2,1)S(1)}, bf16[1,4,256,256]{3,2,1,0:T(8,128)(2,1)}, u32[]{:S(2)}) copy-start(bf16[1,4,256,256]{3,2,1,0:T(8,128)(2,1)} %param.72) | copy-start | bytes 1572868
